TPU v7x, 32 devices: a whole 2x2x4 slice. The times are simulated.
32 devices in a mesh: ep: 8 (over y, x, core), tp: 4 (over z).
Axes of the slice: x: 2, y: 2, z: 4, core: 2. Of those that a mesh axis runs over, the one named last changes fastest.
Arguments:
- tokens: bfloat16 [256, 4096], P('ep', 'tp'), may hold values from -6 to 6
- norm_gains: float32 [2, 4096], replicated, may hold values from 0.1 to 1.9
- router: bfloat16 [2, 4096, 16], replicated, as said below
- w_gate: bfloat16 [2, 16, 4096, 768], P(None, 'ep', None, 'tp'), may hold values from -0.09375 to 0.09375
- w_up: bfloat16 [2, 16, 4096, 768], P(None, 'ep', None, 'tp'), may hold values from -0.09375 to 0.09375
- w_down: bfloat16 [2, 16, 768, 4096], P(None, 'ep', 'tp'), may hold values from -0.21875 to 0.21875
- expert_ids: int32 [2, 256, 8], P(None, 'ep'), may hold values from 0 to 15, all different within a row; in each aligned block of 32 rows (0 to 31, 32 to 63, ...) at most 32 rows name the same one
Outputs:
- hidden_out: bfloat16 [256, 4096], P('ep', 'tp')
Inputs may be any that keep to these rules, and one draw needn't show every extreme that they name: `expert_ids`: each entry names an expert of 0 to 15; the 8 entries of a token differ; among the 32 tokens of one ep index in one layer no expert is named more than 32 times, and in some such blocks one is named exactly 32 times. `router`: entries of order 2 / sqrt(4096); all columns of a layer may share a common added vector with entries of order 50 / sqrt(4096).
All inputs are finite; a program needn't handle non-finite values.
Results may differ from a plain program's by a relative error of at most 0.02.
Values may be sent and summed in bfloat16 or wider, within the bound.
A program may use at most 64 MiB of HBM per device.

v0:
```python
import jax
import jax.numpy as jnp
from jax import lax
from jax.sharding import PartitionSpec as P

TOP = 8
LAYERS = 2
norm_eps = 1e-06


def body(tokens, norm_gains, router, w_gate, w_up, w_down, expert_ids):
    n_tp = lax.axis_size("tp")
    n_ep = lax.axis_size("ep")
    local_width = tokens.shape[1]
    full_width = local_width * n_tp
    rows_dev = tokens.shape[0]
    local_exp = w_gate.shape[1]
    experts = local_exp * n_ep
    capacity = 2 * rows_dev * TOP // experts
    current = tokens
    for layer_idx in range(LAYERS):
        gain = norm_gains[layer_idx]
        weight = router[layer_idx]
        ids = expert_ids[layer_idx]
        normed = None
        whole = lax.all_gather(current, "tp", axis=1, tiled=True)
        wide_rows = whole.astype(jnp.float32)
        square_sum = jnp.sum(wide_rows * wide_rows, axis=1)
        scaled = (wide_rows * gain[None, :]).astype(jnp.bfloat16)
        raw_logits = jnp.dot(scaled, weight, preferred_element_type=jnp.float32)
        inverse = lax.rsqrt(square_sum / full_width + norm_eps)
        normed = (scaled.astype(jnp.float32) * inverse[:, None]).astype(jnp.bfloat16)
        logits = raw_logits * inverse[:, None]
        choose = ids[:, :, None] == lax.iota(jnp.int32, experts)[None, None, :]
        picked = jnp.sum(jnp.where(choose, logits[:, None, :], 0.0), axis=-1)
        gate_probs = jax.nn.softmax(picked, axis=-1)
        onehot = choose.reshape(rows_dev * TOP, experts).astype(jnp.int32)
        earlier = jnp.cumsum(onehot, axis=0) - onehot
        slot_index = jnp.sum(earlier * onehot, axis=1).reshape(rows_dev, TOP)
        slot_key = ids * capacity + slot_index
        slot_hits = slot_key[None, :, :] == lax.iota(jnp.int32, experts * capacity)[:, None, None]
        route_matrix = jnp.any(slot_hits, axis=-1).astype(jnp.bfloat16)
        combine_matrix = jnp.sum(jnp.where(slot_hits, gate_probs[None, :, :], 0.0), axis=-1).T
        outgoing = jnp.dot(route_matrix, normed, preferred_element_type=jnp.float32).astype(
            jnp.bfloat16
        )
        outgoing = outgoing.reshape(n_ep, local_exp * capacity, full_width)
        incoming = lax.all_to_all(outgoing, "ep", split_axis=0, concat_axis=0, tiled=True)
        arrived = incoming.reshape(n_ep, local_exp, capacity, full_width).transpose(1, 0, 2, 3)
        arrived = arrived.reshape(local_exp, n_ep * capacity, full_width)
        gate_proj = jnp.einsum(
            "erd,edf->erf", arrived, w_gate[layer_idx], preferred_element_type=jnp.float32
        )
        up_proj = jnp.einsum(
            "erd,edf->erf", arrived, w_up[layer_idx], preferred_element_type=jnp.float32
        )
        inner = (jax.nn.silu(gate_proj) * up_proj).astype(jnp.bfloat16)
        down_local = w_down[layer_idx]

        def project():
            down_piece = lax.slice_in_dim(down_local, 0, local_width * lax.axis_size("tp"), axis=2)
            return jnp.einsum("erf,efd->der", inner, down_piece, preferred_element_type=jnp.float32)

        summed = lax.psum_scatter(
            project().astype(jnp.bfloat16), "tp", scatter_dimension=0, tiled=True
        ).astype(jnp.float32)
        out_rows = summed.astype(jnp.bfloat16).reshape(local_width, local_exp, n_ep, capacity)
        out_rows = out_rows.transpose(2, 1, 3, 0).reshape(n_ep, local_exp * capacity, local_width)
        returned = lax.all_to_all(out_rows, "ep", split_axis=0, concat_axis=0, tiled=True)
        returned = returned.reshape(experts * capacity, local_width).astype(jnp.float32)
        moe_out = jnp.dot(combine_matrix, returned, precision=lax.Precision.HIGHEST)
        current = (current.astype(jnp.float32) + moe_out).astype(jnp.bfloat16)
    return current


def solution(mesh):
    in_specs = (
        P("ep", "tp"),
        P(),
        P(),
        P(None, "ep", None, "tp"),
        P(None, "ep", None, "tp"),
        P(None, "ep", "tp", None),
        P(None, "ep", None),
    )
    out_specs = P("ep", "tp")
    return jax.shard_map(body, mesh=mesh, in_specs=in_specs, out_specs=out_specs, check_vma=False)
```

profile of v0, /device:TPU:0, one launch (start us, length us, event | category | flops | bytes accessed | tf_op | source)
XLA Modules:
  0.0 376.2 jit_solution(15348728780867839647)
XLA Ops:
  6.5 0.7 fusion.79
  8.8 0.9 fusion.78
  9.6 15.9 %all_gather.6 = bf16[32,4096]{1,0:T(8,128)(2,1)S(1)} all-gather(bf16[32,1024]{1,0:T(8,128)(2,1)} %param.7), channel_id=1, replica_groups=mesh['ep'=8,'tp'=4] {'tp'}, dimensions={1}, use_global_device_ids=true | all-gather | bytes 327680 | tf_op jit(solution)/shard_map/all_gather | solution.py:26
  25.7 1.3 convolution_convert_fusion.3
  27.0 52.8 %all_to_all.20 = bf16[8,64,4096]{2,1,0:T(8,128)(2,1)S(1)} all-to-all(bf16[8,64,4096]{2,1,0:T(8,128)(2,1)S(1)} %bitcast.120), channel_id=1, replica_groups=mesh['ep'=8,'tp'=4] {'ep'}, dimensions={0} | all-to-all | bytes 8388608 | tf_op jit(solution)/shard_map/all_to_all | solution.py:48
  80.3 2.0 copy-done
  82.3 1.5 fusion.10
  83.9 8.8 %fusion = bf16[4096,2,256]{0,2,1:T(8,128)(2,1)} fusion(bf16[2,2,192,4096]{3,2,1,0:T(8,128)(2,1)} %param.12, bf16[2,256,4096]{2,1,0:T(8,128)(2,1)} %bitcast.125, bf16[2,2,4096,192]{2,3,1,0:T(8,128)(2,1)} %param.11, f32[2,256,192]{1,2,0:T(8,128)S(1)} %fusion.10), kind=kOutput, calls=%fused_computation.4 | convolution fusion | flops 1613299712 | bytes 15073280 | tf_op jit(solution)/shard_map/erf,efd->der/dot_general | solution.py:62
  94.1 75.1 %reduce-scatter.3.cloned.1.call-done = bf16[1024,2,256]{0,2,1:T(8,128)(2,1)} async-done(((bf16[4096,2,256]{0,2,1:T(8,128)(2,1)}), bf16[1024,2,256]{0,2,1:T(8,128)(2,1)}) %reduce-scatter.3.cloned.1.call-update) | async-done | bytes 1048592 | tf_op jit(solution)/shard_map/reduce_scatter | solution.py:64
  169.3 2.3 copy.31
  171.6 3.6 all-to-all-start.1
  175.9 14.7 %all-to-all-done.1 = bf16[8,64,1024]{2,1,0:T(8,128)(2,1)S(1)} async-done(((bf16[8,64,1024]{2,1,0:T(8,128)(2,1)}), bf16[8,64,1024]{2,1,0:T(8,128)(2,1)S(1)}, u32[]{:S(2)}, u32[]{:S(2)}) %all-to-all-start.1) | async-done | bytes 1048608 | tf_op jit(solution)/shard_map/all_to_all | solution.py:69
  190.6 0.6 fusion.30
  191.2 14.4 %all_gather.7 = bf16[32,4096]{1,0:T(8,128)(2,1)S(1)} all-gather(bf16[32,1024]{1,0:T(8,128)(2,1)S(1)} %fusion.30), channel_id=1, replica_groups=mesh['ep'=8,'tp'=4] {'tp'}, dimensions={1}, use_global_device_ids=true | all-gather | bytes 327680 | tf_op jit(solution)/shard_map/all_gather | solution.py:26
  205.8 1.3 convolution_convert_fusion.1
  207.1 51.8 %all_to_all.21 = bf16[8,64,4096]{2,1,0:T(8,128)(2,1)S(1)} all-to-all(bf16[8,64,4096]{2,1,0:T(8,128)(2,1)S(1)} %bitcast.122), channel_id=1, replica_groups=mesh['ep'=8,'tp'=4] {'ep'}, dimensions={0} | all-to-all | bytes 8388608 | tf_op jit(solution)/shard_map/all_to_all | solution.py:48
  259.4 2.0 copy-done.1
  261.4 1.5 fusion.5
  262.9 8.8 %fusion.1 = bf16[4096,2,256]{0,2,1:T(8,128)(2,1)} fusion(bf16[2,2,192,4096]{3,2,1,0:T(8,128)(2,1)} %param.12, bf16[2,256,4096]{2,1,0:T(8,128)(2,1)} %bitcast.127, bf16[2,2,4096,192]{2,3,1,0:T(8,128)(2,1)} %param.11, f32[2,256,192]{1,2,0:T(8,128)S(1)} %fusion.5), kind=kOutput, calls=%fused_computation.5 | convolution fusion | flops 1613299712 | bytes 15073280 | tf_op jit(solution)/shard_map/erf,efd->der/dot_general | solution.py:62
  271.7 75.0 %reduce-scatter.5.cloned.1.call-done = bf16[1024,2,256]{0,2,1:T(8,128)(2,1)} async-done(((bf16[4096,2,256]{0,2,1:T(8,128)(2,1)}), bf16[1024,2,256]{0,2,1:T(8,128)(2,1)}) %reduce-scatter.5.cloned.1.call-update) | async-done | bytes 1048592 | tf_op jit(solution)/shard_map/reduce_scatter | solution.py:64
  346.7 2.3 copy.37
  349.0 3.7 all-to-all-start.3
  353.3 14.8 %all-to-all-done.3 = bf16[8,64,1024]{2,1,0:T(8,128)(2,1)S(1)} async-done(((bf16[8,64,1024]{2,1,0:T(8,128)(2,1)}), bf16[8,64,1024]{2,1,0:T(8,128)(2,1)S(1)}, u32[]{:S(2)}, u32[]{:S(2)}) %all-to-all-start.3) | async-done | bytes 1048608 | tf_op jit(solution)/shard_map/all_to_all | solution.py:69
  368.1 1.2 fusion.31
  (64 shorter events, 5.6 us)
Async XLA Ops:
  6.5 162.8 %reduce-scatter.3.cloned.1.call-start = ((), (), s32[]{:S(2)}) async-start(), calls=%async_computation.6 | async-start | bytes 5242880 | tf_op jit(solution)/shard_map/reduce_scatter | solution.py:64
  27.0 55.3 %slice-start = ((s8[6291456]{0:T(1024)(128)(4,1)}), s8[4194304]{0:T(1024)(128)(4,1)S(1)}, s32[]{:S(2)}) async-start(s8[6291456]{0:T(1024)(128)(4,1)} %bitcast.136), calls=%async_computation.8 | async-start | bytes 8388608
  79.8 2.5 slice-start.1
  80.3 2.0 copy-start
  92.6 1.3 copy-start.3
  92.6 98.0 %copy-start.2 = (bf16[32,1024]{1,0:T(8,128)(2,1)S(1)}, bf16[32,1024]{1,0:T(8,128)(2,1)}, u32[]{:S(2)}) copy-start(bf16[32,1024]{1,0:T(8,128)(2,1)} %param.7) | copy-start | bytes 196612
  171.6 19.0 %all-to-all-start.1 = ((bf16[8,64,1024]{2,1,0:T(8,128)(2,1)}), bf16[8,64,1024]{2,1,0:T(8,128)(2,1)S(1)}, u32[]{:S(2)}, u32[]{:S(2)}) async-start(bf16[8,64,1024]{2,1,0:T(8,128)(2,1)} %bitcast.16), calls=%async_computation.2 | async-start | bytes 2097152 | tf_op jit(solution)/shard_map/all_to_all | solution.py:69
  175.2 171.5 %reduce-scatter.5.cloned.1.call-start = ((), (), s32[]{:S(2)}) async-start(), calls=%async_computation.7 | async-start | bytes 5242880 | tf_op jit(solution)/shard_map/reduce_scatter | solution.py:64
  207.1 54.3 %slice-start.2 = ((s8[6291456]{0:T(1024)(128)(4,1)}), s8[4194304]{0:T(1024)(128)(4,1)S(1)}, s32[]{:S(2)}) async-start(s8[6291456]{0:T(1024)(128)(4,1)} %bitcast.138), calls=%async_computation.10 | async-start | bytes 8388608
  258.9 2.5 slice-start.3
  259.4 2.0 copy-start.1
  349.0 19.0 %all-to-all-start.3 = ((bf16[8,64,1024]{2,1,0:T(8,128)(2,1)}), bf16[8,64,1024]{2,1,0:T(8,128)(2,1)S(1)}, u32[]{:S(2)}, u32[]{:S(2)}) async-start(bf16[8,64,1024]{2,1,0:T(8,128)(2,1)} %bitcast.34), calls=%async_computation.5 | async-start | bytes 2097152 | tf_op jit(solution)/shard_map/all_to_all | solution.py:69
Sparse Core Ops, SparseCore 0:
  92.8 76.4 reduce-scatter.2
  271.8 74.8 reduce-scatter.4
where the time goes:
time: 377 us; the launch traced here: 376 us
  waiting for transfers between devices  180 us (48%)
  blocking collectives  135 us (36%)
  matrix products  25.5 us (7%)
  between operations  13.6 us (4%)
  local copies, waits for them, and re-layouts  12.3 us (3%)
  starting transfers between devices  7.32 us (2%)
    reduce_scatter x2, waiting for transfers between devices, body(): lax.psum_scatter(project().astype(jnp.bfloat16), 'tp', scatter_dimension=...  150 us
    all_to_all x2, blocking collectives, body(): lax.all_to_all(outgoing, 'ep', split_axis=0, concat_axis=0, tiled=True)  105 us
    all_gather x2, blocking collectives, body(): whole = lax.all_gather(current, 'tp', axis=1, tiled=True)  30.2 us
    all_to_all x2, waiting for transfers between devices, body(): lax.all_to_all(out_rows, 'ep', split_axis=0, concat_axis=0, tiled=True)  29.5 us
    dot_general x2, matrix products, project(): jnp.einsum('erf,efd->der', inner, down_piece, preferred_element_type=jnp....  17.6 us
  transfers between devices with their start and end apart: 4, of which 4 were waited for; matrix products, arithmetic and copies ran while one was open for 1% of the time, Pallas kernels for 0%

commit v1 on v0

--- a/solution.py
+++ b/solution.py
@@ -2,6 +2,7 @@
 import jax.numpy as jnp
 from jax import lax
 from jax.sharding import PartitionSpec as P
+from jax.lax import all_gather
 
 TOP = 8
 LAYERS = 2
@@ -23,7 +24,12 @@
         weight = router[layer_idx]
         ids = expert_ids[layer_idx]
         normed = None
-        whole = lax.all_gather(current, "tp", axis=1, tiled=True)
+
+        def cards_supply_all(q_in):
+            g_now = all_gather(q_in, axis_name="tp")
+            return jnp.concatenate(g_now, axis=1)
+
+        whole = cards_supply_all(current)
         wide_rows = whole.astype(jnp.float32)
         square_sum = jnp.sum(wide_rows * wide_rows, axis=1)
         scaled = (wide_rows * gain[None, :]).astype(jnp.bfloat16)

time: 377 us -> 378 us (level)
  no operation moved by 1% of the time
where the time goes in v1:
time: 378 us
  waiting for transfers between devices  179 us (47%)
  blocking collectives  135 us (36%)
  matrix products  25.5 us (7%)
  local copies, waits for them, and re-layouts  13.8 us (4%)
  between operations  13.6 us (4%)
  starting transfers between devices  7.35 us (2%)
  other arithmetic  3.83 us (1%)
    reduce_scatter x2, waiting for transfers between devices, body(): lax.psum_scatter(project().astype(jnp.bfloat16), 'tp', scatter_dimension=...  150 us
    all_to_all x2, blocking collectives, body(): lax.all_to_all(outgoing, 'ep', split_axis=0, concat_axis=0, tiled=True)  105 us
    all_gather x2, blocking collectives, cards_supply_all(): g_now = all_gather(q_in, axis_name='tp')  30.2 us
    all_to_all x2, waiting for transfers between devices, body(): lax.all_to_all(out_rows, 'ep', split_axis=0, concat_axis=0, tiled=True)  28.5 us
    dot_general x2, matrix products, project(): jnp.einsum('erf,efd->der', inner, down_piece, preferred_element_type=jnp....  17.6 us
  transfers between devices with their start and end apart: 4, of which 4 were waited for; matrix products, arithmetic and copies ran while one was open for 1% of the time, Pallas kernels for 0%

profile of v1, /device:TPU:0, one launch (start us, length us, event | category | flops | bytes accessed | tf_op | source)
XLA Modules:
  0.0 377.8 jit_solution(2787158290172367113)
XLA Ops:
  6.5 0.7 fusion.74
  7.5 15.9 %all-gather = bf16[128,1024]{1,0:T(8,128)(2,1)S(1)} all-gather(bf16[32,1024]{1,0:T(8,128)(2,1)} %param.7), channel_id=2, replica_groups=mesh['ep'=8,'tp'=4] {'tp'}, dimensions={0}, use_global_device_ids=true | all-gather | bytes 327680 | tf_op jit(solution)/shard_map/all_gather | solution.py:29
  23.4 0.9 slice_reduce_fusion.3
  26.5 1.3 convolution_convert_fusion.3
  27.9 52.8 %all_to_all.20 = bf16[8,64,4096]{2,1,0:T(8,128)(2,1)S(1)} all-to-all(bf16[8,64,4096]{2,1,0:T(8,128)(2,1)S(1)} %bitcast.140), channel_id=1, replica_groups=mesh['ep'=8,'tp'=4] {'ep'}, dimensions={0} | all-to-all | bytes 8388608 | tf_op jit(solution)/shard_map/all_to_all | solution.py:54
  81.2 2.0 copy-done
  83.2 1.5 fusion.10
  84.7 8.8 %fusion = bf16[4096,2,256]{0,2,1:T(8,128)(2,1)} fusion(bf16[2,2,192,4096]{3,2,1,0:T(8,128)(2,1)} %param.12, bf16[2,256,4096]{2,1,0:T(8,128)(2,1)} %bitcast.145, bf16[2,2,4096,192]{2,3,1,0:T(8,128)(2,1)} %param.11, f32[2,256,192]{1,2,0:T(8,128)S(1)} %fusion.10), kind=kOutput, calls=%fused_computation.4 | convolution fusion | flops 1613299712 | bytes 15073280 | tf_op jit(solution)/shard_map/erf,efd->der/dot_general | solution.py:68
  94.8 75.3 %reduce-scatter.3.cloned.1.call-done = bf16[1024,2,256]{0,2,1:T(8,128)(2,1)} async-done(((bf16[4096,2,256]{0,2,1:T(8,128)(2,1)}), bf16[1024,2,256]{0,2,1:T(8,128)(2,1)}) %reduce-scatter.3.cloned.1.call-update) | async-done | bytes 1048592 | tf_op jit(solution)/shard_map/reduce_scatter | solution.py:70
  170.1 2.3 copy.37
  172.4 3.7 all-to-all-start.1
  177.6 13.8 %all-to-all-done.1 = bf16[8,64,1024]{2,1,0:T(8,128)(2,1)S(1)} async-done(((bf16[8,64,1024]{2,1,0:T(8,128)(2,1)}), bf16[8,64,1024]{2,1,0:T(8,128)(2,1)S(1)}, u32[]{:S(2)}, u32[]{:S(2)}) %all-to-all-start.1) | async-done | bytes 1048608 | tf_op jit(solution)/shard_map/all_to_all | solution.py:75
  191.5 0.6 fusion.30
  192.1 14.4 %all-gather.1 = bf16[128,1024]{1,0:T(8,128)(2,1)S(1)} all-gather(bf16[32,1024]{1,0:T(8,128)(2,1)S(1)} %fusion.30), channel_id=3, replica_groups=mesh['ep'=8,'tp'=4] {'tp'}, dimensions={0}, use_global_device_ids=true | all-gather | bytes 327680 | tf_op jit(solution)/shard_map/all_gather | solution.py:29
  207.4 1.3 convolution_convert_fusion.1
  208.7 51.8 %all_to_all.21 = bf16[8,64,4096]{2,1,0:T(8,128)(2,1)S(1)} all-to-all(bf16[8,64,4096]{2,1,0:T(8,128)(2,1)S(1)} %bitcast.141), channel_id=1, replica_groups=mesh['ep'=8,'tp'=4] {'ep'}, dimensions={0} | all-to-all | bytes 8388608 | tf_op jit(solution)/shard_map/all_to_all | solution.py:54
  261.0 2.0 copy-done.1
  263.0 1.5 fusion.5
  264.5 8.8 %fusion.1 = bf16[4096,2,256]{0,2,1:T(8,128)(2,1)} fusion(bf16[2,2,192,4096]{3,2,1,0:T(8,128)(2,1)} %param.12, bf16[2,256,4096]{2,1,0:T(8,128)(2,1)} %bitcast.147, bf16[2,2,4096,192]{2,3,1,0:T(8,128)(2,1)} %param.11, f32[2,256,192]{1,2,0:T(8,128)S(1)} %fusion.5), kind=kOutput, calls=%fused_computation.5 | convolution fusion | flops 1613299712 | bytes 15073280 | tf_op jit(solution)/shard_map/erf,efd->der/dot_general | solution.py:68
  273.3 75.0 %reduce-scatter.5.cloned.1.call-done = bf16[1024,2,256]{0,2,1:T(8,128)(2,1)} async-done(((bf16[4096,2,256]{0,2,1:T(8,128)(2,1)}), bf16[1024,2,256]{0,2,1:T(8,128)(2,1)}) %reduce-scatter.5.cloned.1.call-update) | async-done | bytes 1048592 | tf_op jit(solution)/shard_map/reduce_scatter | solution.py:70
  348.4 2.3 copy.45
  350.7 3.7 all-to-all-start.3
  355.0 14.7 %all-to-all-done.3 = bf16[8,64,1024]{2,1,0:T(8,128)(2,1)S(1)} async-done(((bf16[8,64,1024]{2,1,0:T(8,128)(2,1)}), bf16[8,64,1024]{2,1,0:T(8,128)(2,1)S(1)}, u32[]{:S(2)}, u32[]{:S(2)}) %all-to-all-start.3) | async-done | bytes 1048608 | tf_op jit(solution)/shard_map/all_to_all | solution.py:75
  369.7 1.2 fusion.31
  (74 shorter events, 7.9 us)
Async XLA Ops:
  6.5 163.6 %reduce-scatter.3.cloned.1.call-start = ((), (), s32[]{:S(2)}) async-start(), calls=%async_computation.6 | async-start | bytes 5242880 | tf_op jit(solution)/shard_map/reduce_scatter | solution.py:70
  27.9 55.3 %slice-start = ((s8[6291456]{0:T(1024)(128)(4,1)}), s8[4194304]{0:T(1024)(128)(4,1)S(1)}, s32[]{:S(2)}) async-start(s8[6291456]{0:T(1024)(128)(4,1)} %bitcast.164), calls=%async_computation.8 | async-start | bytes 8388608
  80.7 2.5 slice-start.1
  81.2 2.0 copy-start
  93.5 0.9 copy-start.3
  93.5 98.0 %copy-start.2 = (bf16[32,1024]{1,0:T(8,128)(2,1)S(1)}, bf16[32,1024]{1,0:T(8,128)(2,1)}, u32[]{:S(2)}) copy-start(bf16[32,1024]{1,0:T(8,128)(2,1)} %param.7) | copy-start | bytes 196612
  172.4 19.0 %all-to-all-start.1 = ((bf16[8,64,1024]{2,1,0:T(8,128)(2,1)}), bf16[8,64,1024]{2,1,0:T(8,128)(2,1)S(1)}, u32[]{:S(2)}, u32[]{:S(2)}) async-start(bf16[8,64,1024]{2,1,0:T(8,128)(2,1)} %bitcast.20), calls=%async_computation.2 | async-start | bytes 2097152 | tf_op jit(solution)/shard_map/all_to_all | solution.py:75
  176.1 172.3 %reduce-scatter.5.cloned.1.call-start = ((), (), s32[]{:S(2)}) async-start(), calls=%async_computation.7 | async-start | bytes 5242880 | tf_op jit(solution)/shard_map/reduce_scatter | solution.py:70
  208.7 54.3 %slice-start.2 = ((s8[6291456]{0:T(1024)(128)(4,1)}), s8[4194304]{0:T(1024)(128)(4,1)S(1)}, s32[]{:S(2)}) async-start(s8[6291456]{0:T(1024)(128)(4,1)} %bitcast.166), calls=%async_computation.10 | async-start | bytes 8388608
  260.5 2.5 slice-start.3
  261.0 2.0 copy-start.1
  350.7 19.0 %all-to-all-start.3 = ((bf16[8,64,1024]{2,1,0:T(8,128)(2,1)}), bf16[8,64,1024]{2,1,0:T(8,128)(2,1)S(1)}, u32[]{:S(2)}, u32[]{:S(2)}) async-start(bf16[8,64,1024]{2,1,0:T(8,128)(2,1)} %bitcast.42), calls=%async_computation.5 | async-start | bytes 2097152 | tf_op jit(solution)/shard_map/all_to_all | solution.py:75
Sparse Core Ops, SparseCore 0:
  93.6 76.4 reduce-scatter.2
  273.5 74.8 reduce-scatter.4
